TPU v7x, 32 devices: a whole 2x2x4 slice. The times are simulated.
32 devices in a mesh: grp: 2 (over core), gx: 4 (over z), gy: 4 (over y, x).
Axes of the slice: x: 2, y: 2, z: 4, core: 2. Of those that a mesh axis runs over, the one named last changes fastest.
Arguments:
- coarse_ez: float32 [256, 1024], P('gx', ('grp', 'gy')), may hold values from -6 to 6
- coarse_hx: float32 [256, 1024], P('gx', ('grp', 'gy')), may hold values from -6 to 6
- coarse_hy: float32 [256, 1024], P('gx', ('grp', 'gy')), may hold values from -6 to 6
- coarse_ids: int32 [256, 1024], P('gx', ('grp', 'gy')), may hold values from 0 to 7
- mat_eps: float32 [8], replicated, may hold values from 1 to 12
- mat_sig: float32 [8], replicated, may hold values from 0 to 0.5
- fine_ez: float32 [4, 8, 32, 2304], P(None, ('grp', 'gy'), 'gx'), may hold values from -6 to 6
- fine_hx: float32 [4, 8, 32, 2304], P(None, ('grp', 'gy'), 'gx'), may hold values from -6 to 6
- fine_hy: float32 [4, 8, 32, 2304], P(None, ('grp', 'gy'), 'gx'), may hold values from -6 to 6
- fine_ids: int32 [4, 8, 32, 2304], P(None, ('grp', 'gy'), 'gx'), may hold values from 0 to 7
- boxes: int32 [4, 8, 32, 4], P('gx', ('grp', 'gy')), may hold values from 1 to 14, as said below
- src_cells: int32 [4], replicated, may hold values from 0 to 262143
- src_wave: float32 [3, 4], replicated, may hold values from -6 to 6
- rcv_cells: int32 [128], replicated, may hold values from 0 to 262143
Outputs:
- end_ez: float32 [256, 1024], P('gx', ('grp', 'gy'))
- end_hx: float32 [256, 1024], P('gx', ('grp', 'gy'))
- end_hy: float32 [256, 1024], P('gx', ('grp', 'gy'))
- end_fine_ez: float32 [4, 8, 32, 2304], P(None, ('grp', 'gy'), 'gx')
- end_fine_hx: float32 [4, 8, 32, 2304], P(None, ('grp', 'gy'), 'gx')
- end_fine_hy: float32 [4, 8, 32, 2304], P(None, ('grp', 'gy'), 'gx')
- traces: float32 [3, 128], replicated
Inputs may be any that keep to these rules, and one draw needn't show every extreme that they name: `boxes`: each box lies one cell or more inside its tile: corner + size <= 15; sizes are 4 to 14, drawn independently for every subgrid.
All inputs are finite; a program needn't handle non-finite values.
Results may differ from a plain program's by a relative error of at most 0.00011.
Values sent between devices are 32-bit elements; how exact they have to be, the bound alone decides.
No kernel may reach another device: no remote copies, remote signals or barrier semaphores. Data moves between devices by JAX's collectives and lax.ppermute only.
A program may use at most 64 MiB of HBM per device.

v0:
```python
import jax
import jax.numpy as jnp
from jax import lax
from jax.sharding import PartitionSpec as P

TILE = 16
STEPS = 3
COURANT = 0.5
HCOEF = 0.5


def passed_along(value, axis, steps):
    count = lax.axis_size(axis)
    initial, last = (max(0, -steps), min(count, count - steps))
    return lax.ppermute(value, axis, [(source, source + steps) for source in range(initial, last)])


def coefficients(ids, eps_table, sig_table, ratio):
    damp = jnp.zeros(ids.shape, jnp.float32)
    gain = jnp.zeros(ids.shape, jnp.float32)
    for material in range(eps_table.shape[0]):
        loss = sig_table[material] / (eps_table[material] * ratio)
        hit = ids == material
        damp = jnp.where(hit, (1.0 - loss) / (1.0 + loss), damp)
        gain = jnp.where(hit, COURANT / (eps_table[material] * (1.0 + loss)), gain)
    return (damp, gain)


def box_masks(boxes, cells, scale):
    coarse_of = jnp.arange(cells, dtype=jnp.int32) // scale
    low_i = boxes[..., 0:1]
    low_j = boxes[..., 1:2]
    high_i = low_i + boxes[..., 2:3]
    high_j = low_j + boxes[..., 3:4]
    rows_in = (coarse_of >= low_i) & (coarse_of < high_i)
    cols_in = (coarse_of >= low_j) & (coarse_of < high_j)
    rows_mid = (coarse_of > low_i) & (coarse_of < high_i - 1)
    cols_mid = (coarse_of > low_j) & (coarse_of < high_j - 1)
    inbox = rows_in[..., :, None] & cols_in[..., None, :]
    middle = rows_mid[..., :, None] & cols_mid[..., None, :]
    return (inbox, middle)


def flat_masks(boxes):
    width = TILE * 3
    index = jnp.arange(width * width, dtype=jnp.int32)
    coarse_i = index // width // 3
    coarse_j = index % width // 3
    low_i = boxes[:, 0:1]
    low_j = boxes[:, 1:2]
    high_i = low_i + boxes[:, 2:3]
    high_j = low_j + boxes[:, 3:4]
    inbox = (coarse_i >= low_i) & (coarse_i < high_i) & (coarse_j >= low_j) & (coarse_j < high_j)
    middle = (
        (coarse_i > low_i) & (coarse_i < high_i - 1) & (coarse_j > low_j) & (coarse_j < high_j - 1)
    )
    return (inbox, middle)


def spread_table():
    width = TILE * 3
    index = jnp.arange(width * width, dtype=jnp.int32)
    owner = index // width // 3 * TILE + index % width // 3
    return (jnp.arange(TILE * TILE, dtype=jnp.int32)[:, None] == owner[None, :]).astype(jnp.float32)


def to_flat_tiles(field):
    rows, cols = field.shape
    along_x = rows // TILE
    along_y = cols // TILE
    shaped = field.reshape(along_x, TILE, along_y, TILE).transpose(0, 2, 1, 3)
    return shaped.reshape(1, 1, along_x * along_y, TILE * TILE)


def from_tiles(tiles, block_rows, block_cols):
    along_x = block_rows // TILE
    along_y = block_cols // TILE
    shaped = tiles.reshape(along_x, along_y, TILE, TILE).transpose(0, 2, 1, 3)
    return shaped.reshape(block_rows, block_cols)


def pad_last(array, before, after):
    widths = [(0, 0)] * (array.ndim - 1) + [(before, after)]
    return jnp.pad(array, widths)


def fine_substep(fine_ez, fine_hx, fine_hy, damp, gain, inbox, middle, border, cycle_value):
    width = TILE * 3
    column = jnp.arange(width * width, dtype=jnp.int32) % width
    ez_next_col = jnp.where(column < width - 1, pad_last(fine_ez[..., 1:], 0, 1), 0.0)
    ez_next_row = pad_last(fine_ez[..., width:], 0, width)
    fine_hx = jnp.where(inbox, fine_hx - HCOEF * (ez_next_col - fine_ez), 0.0)
    fine_hy = jnp.where(inbox, fine_hy + HCOEF * (ez_next_row - fine_ez), 0.0)
    hy_prev = pad_last(fine_hy[..., :-width], width, 0)
    hx_prev = jnp.where(column > 0, pad_last(fine_hx[..., :-1], 1, 0), 0.0)
    curl = fine_hy - hy_prev - (fine_hx - hx_prev)
    inner = damp * fine_ez + gain * curl
    fine_ez = jnp.where(middle, inner, jnp.where(border, cycle_value, 0.0))
    return (fine_ez, fine_hx, fine_hy)


def fine_round(
    fine_ez, fine_hx, fine_hy, damp, gain, inbox, middle, border, old_tiles, new_tiles, spread
):
    for sub in range(1, 4):
        weight = sub / 3.0
        mixed = (1.0 - weight) * old_tiles + weight * new_tiles
        cycle_value = jnp.dot(
            mixed, spread, precision=lax.Precision.HIGHEST, preferred_element_type=jnp.float32
        )
        fine_ez, fine_hx, fine_hy = fine_substep(
            fine_ez, fine_hx, fine_hy, damp, gain, inbox, middle, border, cycle_value
        )
    return (fine_ez, fine_hx, fine_hy)


def coarse_magnetic(ez, hx, hy):
    below = passed_along(ez[:1, :], "gx", -1)
    beside = passed_along(ez[:, :1], ("grp", "gy"), -1)
    ez_next_row = jnp.concatenate([ez[1:, :], below], axis=0)
    ez_next_col = jnp.concatenate([ez[:, 1:], beside], axis=1)
    hx = hx - HCOEF * (ez_next_col - ez)
    hy = hy + HCOEF * (ez_next_row - ez)
    above = passed_along(hy[-1:, :], "gx", 1)
    before = passed_along(hx[:, -1:], ("grp", "gy"), 1)
    hy_prev = jnp.concatenate([above, hy[:-1, :]], axis=0)
    hx_prev = jnp.concatenate([before, hx[:, :-1]], axis=1)
    curl = hy - hy_prev - (hx - hx_prev)
    return (hx, hy, curl)


def shards(
    coarse_ez,
    coarse_hx,
    coarse_hy,
    coarse_ids,
    mat_eps,
    mat_sig,
    fine_ez,
    fine_hx,
    fine_hy,
    fine_ids,
    boxes,
    src_cells,
    src_wave,
    rcv_cells,
):
    rows, cols = coarse_ez.shape
    fine_shape = fine_ez.shape
    flat_cells = fine_shape[-1]
    means_shape = fine_shape[:-1] + (TILE * TILE,)
    row_start = lax.axis_index("gx") * rows
    col_start = lax.axis_index(("grp", "gy")) * cols
    all_cols = cols * lax.axis_size(("grp", "gy"))
    spread = spread_table()
    damp, gain = coefficients(coarse_ids, mat_eps, mat_sig, 1.0)
    fine_damp, fine_gain = coefficients(fine_ids.reshape(-1, flat_cells), mat_eps, mat_sig, 3.0)
    owned_boxes = lax.all_to_all(boxes, "gx", split_axis=2, concat_axis=0, tiled=True).reshape(
        -1, 4
    )
    inbox, middle = flat_masks(owned_boxes)
    border = inbox & jnp.logical_not(middle)
    coarse_mid = from_tiles(box_masks(boxes, TILE, 1)[1], rows, cols)
    src_rows = (
        jnp.arange(rows, dtype=jnp.int32)[None, :] == (src_cells // all_cols - row_start)[:, None]
    ).astype(jnp.float32)
    src_cols = (
        jnp.arange(cols, dtype=jnp.int32)[None, :] == (src_cells % all_cols - col_start)[:, None]
    ).astype(jnp.float32)
    rcv_rows = (
        jnp.arange(rows, dtype=jnp.int32)[None, :] == (rcv_cells // all_cols - row_start)[:, None]
    ).astype(jnp.float32)
    rcv_cols = (
        jnp.arange(cols, dtype=jnp.int32)[None, :] == (rcv_cells % all_cols - col_start)[:, None]
    ).astype(jnp.float32)
    ez, hx, hy = (coarse_ez, coarse_hx, coarse_hy)
    field_ez = fine_ez.reshape(-1, flat_cells)
    field_hx = fine_hx.reshape(-1, flat_cells)
    field_hy = fine_hy.reshape(-1, flat_cells)
    held = lax.all_to_all(to_flat_tiles(ez), "gx", split_axis=2, concat_axis=0, tiled=True).reshape(
        -1, TILE * TILE
    )
    samples = []
    for step in range(STEPS):
        hx, hy, curl = coarse_magnetic(ez, hx, hy)
        weighted = src_rows * src_wave[step][:, None]
        drive = jnp.dot(
            weighted.T,
            src_cols,
            precision=lax.Precision.HIGHEST,
            preferred_element_type=jnp.float32,
        )
        new = damp * ez + gain * curl + drive
        old_tiles = held
        new_tiles = lax.all_to_all(
            to_flat_tiles(new), "gx", split_axis=2, concat_axis=0, tiled=True
        ).reshape(-1, TILE * TILE)
        held = new_tiles
        field_ez, field_hx, field_hy = fine_round(
            field_ez,
            field_hx,
            field_hy,
            fine_damp,
            fine_gain,
            inbox,
            middle,
            border,
            old_tiles,
            new_tiles,
            spread,
        )
        sums = lax.dot_general(
            field_ez,
            spread,
            (((1,), (1,)), ((), ())),
            precision=lax.Precision.HIGHEST,
            preferred_element_type=jnp.float32,
        )
        means = (sums / 9.0).reshape(means_shape)
        back = lax.all_to_all(means, "gx", split_axis=0, concat_axis=2, tiled=True)
        ez = jnp.where(coarse_mid, from_tiles(back, rows, cols), new)
        picked = jnp.dot(
            rcv_rows, ez, precision=lax.Precision.HIGHEST, preferred_element_type=jnp.float32
        )
        samples.append(jnp.sum(picked * rcv_cols, axis=1))
    traces = lax.psum(jnp.stack(samples), ("grp", "gx", "gy"))
    return (
        ez,
        hx,
        hy,
        field_ez.reshape(fine_shape),
        field_hx.reshape(fine_shape),
        field_hy.reshape(fine_shape),
        traces,
    )


def solution(mesh):
    placed = (
        P("gx", ("grp", "gy")),
        P("gx", ("grp", "gy")),
        P("gx", ("grp", "gy")),
        P("gx", ("grp", "gy")),
        P(),
        P(),
        P(None, ("grp", "gy"), "gx", None),
        P(None, ("grp", "gy"), "gx", None),
        P(None, ("grp", "gy"), "gx", None),
        P(None, ("grp", "gy"), "gx", None),
        P("gx", ("grp", "gy"), None, None),
        P(),
        P(),
        P(),
    )
    return jax.shard_map(
        shards,
        mesh=mesh,
        in_specs=placed,
        out_specs=(
            P("gx", ("grp", "gy")),
            P("gx", ("grp", "gy")),
            P("gx", ("grp", "gy")),
            P(None, ("grp", "gy"), "gx", None),
            P(None, ("grp", "gy"), "gx", None),
            P(None, ("grp", "gy"), "gx", None),
            P(),
        ),
        check_vma=False,
    )
```

profile of v0, /device:TPU:0, one launch (start us, length us, event | category | flops | bytes accessed | tf_op | source)
XLA Modules:
  0.0 221.0 jit_solution(844649320013483524)
XLA Ops:
  2.1 6.3 %all-to-all-start = ((s32[1,1,32,4]{3,1,0,2:T(1,128)}), s32[1,1,32,4]{3,1,0,2:T(1,128)S(1)}, u32[]{:S(2)}, u32[]{:S(2)}) async-start(s32[1,1,32,4]{3,1,0,2:T(1,128)} %copy.34), calls=%async_computation | async-start | bytes 32768 | tf_op jit(solution)/shard_map/all_to_all | solution.py:158
  51.5 4.6 %collective-permute-start.1 = (f32[1,128]{1,0:T(1,128)S(1)}, f32[1,128]{1,0:T(1,128)S(1)}, u32[]{:S(2)}, u32[]{:S(2)}) collective-permute-start(f32[1,128]{1,0:T(1,128)S(1)} %slice.384), channel_id=1, source_target_pairs={{0,4},{4,8},{8,12},{1,5},{5,9},{9,13},{2,6},{6,10},{10,14},{3,7},{... | collective-permute-start | bytes 1544 | tf_op jit(solution)/shard_map/ppermute | solution.py:15
  56.1 4.6 %collective-permute-start.3 = (f32[64,1]{1,0:T(8,128)S(1)}, f32[64,1]{1,0:T(8,128)S(1)}, u32[]{:S(2)}, u32[]{:S(2)}) collective-permute-start(f32[64,1]{1,0:T(8,128)S(1)} %slice.386), channel_id=1, source_target_pairs={{0,1},{1,2},{2,3},{3,16},{16,17},{17,18},{18,19},{4,5},{5,6},{6,7}... | collective-permute-start | bytes 776 | tf_op jit(solution)/shard_map/ppermute | solution.py:15
  60.7 4.2 %all-to-all-start.1 = ((f32[1,1,32,256]{3,1,0,2:T(1,128)}), f32[1,1,32,256]{3,1,0,2:T(1,128)S(1)}, u32[]{:S(2)}, u32[]{:S(2)}) async-start(f32[1,1,32,256]{3,1,0,2:T(1,128)} %reshape.417), calls=%async_computation.1 | async-start | bytes 65536 | tf_op jit(solution)/shard_map/all_to_all | solution.py:180
  66.3 4.3 %all-to-all-done.1 = f32[1,1,32,256]{3,1,0,2:T(1,128)S(1)} async-done(((f32[1,1,32,256]{3,1,0,2:T(1,128)}), f32[1,1,32,256]{3,1,0,2:T(1,128)S(1)}, u32[]{:S(2)}, u32[]{:S(2)}) %all-to-all-start.1) | async-done | bytes 32800 | tf_op jit(solution)/shard_map/all_to_all | solution.py:180
  70.5 3.3 %all-to-all-start.2 = ((f32[1,1,32,256]{3,1,0,2:T(1,128)}), f32[1,1,32,256]{3,1,0,2:T(1,128)S(1)}, u32[]{:S(2)}, u32[]{:S(2)}) async-start(f32[1,1,32,256]{3,1,0,2:T(1,128)} %reshape.418), calls=%async_computation.2 | async-start | bytes 65536 | tf_op jit(solution)/shard_map/all_to_all | solution.py:195
  74.1 5.3 %all-to-all-done.2 = f32[1,1,32,256]{3,1,0,2:T(1,128)S(1)} async-done(((f32[1,1,32,256]{3,1,0,2:T(1,128)}), f32[1,1,32,256]{3,1,0,2:T(1,128)S(1)}, u32[]{:S(2)}, u32[]{:S(2)}) %all-to-all-start.2) | async-done | bytes 32800 | tf_op jit(solution)/shard_map/all_to_all | solution.py:195
  83.8 1.8 fusion.28
  85.6 3.3 %all-to-all-start.3 = ((f32[4,1,8,256]{3,2,1,0:T(8,128)}), f32[4,1,8,256]{3,2,1,0:T(8,128)S(1)}, u32[]{:S(2)}, u32[]{:S(2)}) async-start(f32[4,1,8,256]{3,2,1,0:T(8,128)} %fusion.28), calls=%async_computation.3 | async-start | bytes 65536 | tf_op jit(solution)/shard_map/all_to_all | solution.py:220
  89.2 5.3 %all-to-all-done.3 = f32[4,1,8,256]{3,2,1,0:T(8,128)S(1)} async-done(((f32[4,1,8,256]{3,2,1,0:T(8,128)}), f32[4,1,8,256]{3,2,1,0:T(8,128)S(1)}, u32[]{:S(2)}, u32[]{:S(2)}) %all-to-all-start.3) | async-done | bytes 32800 | tf_op jit(solution)/shard_map/all_to_all | solution.py:220
  97.6 4.8 %collective-permute-done.6 = f32[64,1]{1,0:T(8,128)S(1)} collective-permute-done((f32[64,1]{1,0:T(8,128)S(1)}, f32[64,1]{1,0:T(8,128)S(1)}, u32[]{:S(2)}, u32[]{:S(2)}) %collective-permute-start.6) | collective-permute-done | bytes 288 | tf_op jit(solution)/shard_map/ppermute | solution.py:15
  102.5 4.5 %collective-permute-start.5 = (f32[1,128]{1,0:T(1,128)S(1)}, f32[1,128]{1,0:T(1,128)S(1)}, u32[]{:S(2)}, u32[]{:S(2)}) collective-permute-start(f32[1,128]{1,0:T(1,128)S(1)} %slice.402), channel_id=1, source_target_pairs={{0,4},{4,8},{8,12},{1,5},{5,9},{9,13},{2,6},{6,10},{10,14},{3,7},{... | collective-permute-start | bytes 1544 | tf_op jit(solution)/shard_map/ppermute | solution.py:15
  107.1 4.8 %collective-permute-start.7 = (f32[64,1]{1,0:T(8,128)S(1)}, f32[64,1]{1,0:T(8,128)S(1)}, u32[]{:S(2)}, u32[]{:S(2)}) collective-permute-start(f32[64,1]{1,0:T(8,128)S(1)} %slice.406), channel_id=1, source_target_pairs={{0,1},{1,2},{2,3},{3,16},{16,17},{17,18},{18,19},{4,5},{5,6},{6,7}... | collective-permute-start | bytes 776 | tf_op jit(solution)/shard_map/ppermute | solution.py:15
  114.8 3.4 %all-to-all-start.4 = ((f32[1,1,32,256]{3,1,0,2:T(1,128)}), f32[1,1,32,256]{3,1,0,2:T(1,128)S(1)}, u32[]{:S(2)}, u32[]{:S(2)}) async-start(f32[1,1,32,256]{3,1,0,2:T(1,128)} %reshape.419), calls=%async_computation.4 | async-start | bytes 65536 | tf_op jit(solution)/shard_map/all_to_all | solution.py:195
  118.5 5.2 %all-to-all-done.4 = f32[1,1,32,256]{3,1,0,2:T(1,128)S(1)} async-done(((f32[1,1,32,256]{3,1,0,2:T(1,128)}), f32[1,1,32,256]{3,1,0,2:T(1,128)S(1)}, u32[]{:S(2)}, u32[]{:S(2)}) %all-to-all-start.4) | async-done | bytes 32800 | tf_op jit(solution)/shard_map/all_to_all | solution.py:195
  129.3 8.0 %all_to_all.32 = f32[4,1,8,256]{3,2,1,0:T(8,128)S(1)} all-to-all(f32[4,1,8,256]{3,2,1,0:T(8,128)S(1)} %fusion.30), channel_id=1, replica_groups=mesh['grp'=2,'gx'=4,'gy'=4] {'gx'}, dimensions={0} | all-to-all | bytes 65536 | tf_op jit(solution)/shard_map/all_to_all | solution.py:220
  140.4 3.4 %collective-permute-done.10 = f32[64,1]{1,0:T(8,128)S(1)} collective-permute-done((f32[64,1]{1,0:T(8,128)S(1)}, f32[64,1]{1,0:T(8,128)S(1)}, u32[]{:S(2)}, u32[]{:S(2)}) %collective-permute-start.10) | collective-permute-done | bytes 288 | tf_op jit(solution)/shard_map/ppermute | solution.py:15
  144.6 2.6 %collective-permute-start.9 = (f32[1,128]{1,0:T(1,128)S(1)}, f32[1,128]{1,0:T(1,128)S(1)}, u32[]{:S(2)}, u32[]{:S(2)}) collective-permute-start(f32[1,128]{1,0:T(1,128)S(1)} %slice.422), channel_id=1, source_target_pairs={{0,4},{4,8},{8,12},{1,5},{5,9},{9,13},{2,6},{6,10},{10,14},{3,7},{... | collective-permute-start | bytes 1544 | tf_op jit(solution)/shard_map/ppermute | solution.py:15
  147.3 4.8 %collective-permute-start.11 = (f32[64,1]{1,0:T(8,128)S(1)}, f32[64,1]{1,0:T(8,128)S(1)}, u32[]{:S(2)}, u32[]{:S(2)}) collective-permute-start(f32[64,1]{1,0:T(8,128)S(1)} %slice.426), channel_id=1, source_target_pairs={{0,1},{1,2},{2,3},{3,16},{16,17},{17,18},{18,19},{4,5},{5,6},{6,7}... | collective-permute-start | bytes 776 | tf_op jit(solution)/shard_map/ppermute | solution.py:15
  155.0 3.3 %all-to-all-start.6 = ((f32[1,1,32,256]{3,1,0,2:T(1,128)}), f32[1,1,32,256]{3,1,0,2:T(1,128)S(1)}, u32[]{:S(2)}, u32[]{:S(2)}) async-start(f32[1,1,32,256]{3,1,0,2:T(1,128)} %reshape.420), calls=%async_computation.6 | async-start | bytes 65536 | tf_op jit(solution)/shard_map/all_to_all | solution.py:195
  158.6 5.4 %all-to-all-done.6 = f32[1,1,32,256]{3,1,0,2:T(1,128)S(1)} async-done(((f32[1,1,32,256]{3,1,0,2:T(1,128)}), f32[1,1,32,256]{3,1,0,2:T(1,128)S(1)}, u32[]{:S(2)}, u32[]{:S(2)}) %all-to-all-start.6) | async-done | bytes 32800 | tf_op jit(solution)/shard_map/all_to_all | solution.py:195
  170.2 3.3 %all-to-all-start.7 = ((f32[4,1,8,256]{3,2,1,0:T(8,128)}), f32[4,1,8,256]{3,2,1,0:T(8,128)S(1)}, u32[]{:S(2)}, u32[]{:S(2)}) async-start(f32[4,1,8,256]{3,2,1,0:T(8,128)} %fusion.32), calls=%async_computation.7 | async-start | bytes 65536 | tf_op jit(solution)/shard_map/all_to_all | solution.py:220
  173.8 5.3 %all-to-all-done.7 = f32[4,1,8,256]{3,2,1,0:T(8,128)S(1)} async-done(((f32[4,1,8,256]{3,2,1,0:T(8,128)}), f32[4,1,8,256]{3,2,1,0:T(8,128)S(1)}, u32[]{:S(2)}, u32[]{:S(2)}) %all-to-all-start.7) | async-done | bytes 32800 | tf_op jit(solution)/shard_map/all_to_all | solution.py:220
  179.8 41.1 %psum.7 = f32[3,128]{1,0:T(4,128)} all-reduce(f32[3,128]{1,0:T(4,128)S(1)} %pad_maximum_fusion), channel_id=1, replica_groups=mesh['grp'=2,'gx'=4,'gy'=4] {'grp','gx','gy'}, use_global_device_ids=true, to_apply=%region_3.4 | all-reduce | flops 384 | bytes 3072 | tf_op jit(solution)/shard_map/psum | solution.py:226
  (166 shorter events, 45.1 us)
Async XLA Ops:
  0.6 46.8 %copy-start.13 = (f32[3,4]{1,0:T(4,128)S(1)}, f32[3,4]{1,0:T(4,128)}, u32[]{:S(2)}) copy-start(f32[3,4]{1,0:T(4,128)} %param.26) | copy-start | bytes 148
  0.6 46.9 %copy-start.14 = (s32[4]{0:T(128)S(1)}, s32[4]{0:T(128)}, u32[]{:S(2)}) copy-start(s32[4]{0:T(128)} %param.25) | copy-start | bytes 52
  0.7 47.0 %copy-start.4 = (s32[4,1,8,2304]{3,2,1,0:T(8,128)S(1)}, s32[4,1,8,2304]{3,2,1,0:T(8,128)}, u32[]{:S(2)}) copy-start(s32[4,1,8,2304]{3,2,1,0:T(8,128)} %param.23) | copy-start | bytes 884740
  2.1 58.6 %all-to-all-start = ((s32[1,1,32,4]{3,1,0,2:T(1,128)}), s32[1,1,32,4]{3,1,0,2:T(1,128)S(1)}, u32[]{:S(2)}, u32[]{:S(2)}) async-start(s32[1,1,32,4]{3,1,0,2:T(1,128)} %copy.34), calls=%async_computation | async-start | bytes 32768 | tf_op jit(solution)/shard_map/all_to_all | solution.py:158
  8.4 42.9 %collective-permute-start.2 = (f32[64,1]{1,0:T(8,128)}, f32[64,1]{1,0:T(8,128)S(1)}, u32[]{:S(2)}, u32[]{:S(2)}) collective-permute-start(f32[64,1]{1,0:T(8,128)} %bitcast.267), channel_id=1, source_target_pairs={{1,0},{2,1},{3,2},{16,3},{17,16},{18,17},{19,18},{5,4},{6,5},{7,6}... | collective-permute-start | bytes 776 | tf_op jit(solution)/shard_map/ppermute | solution.py:15
  10.4 41.0 %collective-permute-start = (f32[1,128]{1,0:T(1,128)S(1)}, f32[1,128]{1,0:T(1,128)S(1)}, u32[]{:S(2)}, u32[]{:S(2)}) collective-permute-start(f32[1,128]{1,0:T(1,128)S(1)} %slice.322), channel_id=1, source_target_pairs={{4,0},{8,4},{12,8},{5,1},{9,5},{13,9},{6,2},{10,6},{14,10},{7,3},{... | collective-permute-start | bytes 1544 | tf_op jit(solution)/shard_map/ppermute | solution.py:15
  51.5 13.5 %collective-permute-start.1 = (f32[1,128]{1,0:T(1,128)S(1)}, f32[1,128]{1,0:T(1,128)S(1)}, u32[]{:S(2)}, u32[]{:S(2)}) collective-permute-start(f32[1,128]{1,0:T(1,128)S(1)} %slice.384), channel_id=1, source_target_pairs={{0,4},{4,8},{8,12},{1,5},{5,9},{9,13},{2,6},{6,10},{10,14},{3,7},{... | collective-permute-start | bytes 1544 | tf_op jit(solution)/shard_map/ppermute | solution.py:15
  56.1 8.9 %collective-permute-start.3 = (f32[64,1]{1,0:T(8,128)S(1)}, f32[64,1]{1,0:T(8,128)S(1)}, u32[]{:S(2)}, u32[]{:S(2)}) collective-permute-start(f32[64,1]{1,0:T(8,128)S(1)} %slice.386), channel_id=1, source_target_pairs={{0,1},{1,2},{2,3},{3,16},{16,17},{17,18},{18,19},{4,5},{5,6},{6,7}... | collective-permute-start | bytes 776 | tf_op jit(solution)/shard_map/ppermute | solution.py:15
  60.7 9.9 %all-to-all-start.1 = ((f32[1,1,32,256]{3,1,0,2:T(1,128)}), f32[1,1,32,256]{3,1,0,2:T(1,128)S(1)}, u32[]{:S(2)}, u32[]{:S(2)}) async-start(f32[1,1,32,256]{3,1,0,2:T(1,128)} %reshape.417), calls=%async_computation.1 | async-start | bytes 65536 | tf_op jit(solution)/shard_map/all_to_all | solution.py:180
  70.5 8.9 %all-to-all-start.2 = ((f32[1,1,32,256]{3,1,0,2:T(1,128)}), f32[1,1,32,256]{3,1,0,2:T(1,128)S(1)}, u32[]{:S(2)}, u32[]{:S(2)}) async-start(f32[1,1,32,256]{3,1,0,2:T(1,128)} %reshape.418), calls=%async_computation.2 | async-start | bytes 65536 | tf_op jit(solution)/shard_map/all_to_all | solution.py:195
  85.6 8.9 %all-to-all-start.3 = ((f32[4,1,8,256]{3,2,1,0:T(8,128)}), f32[4,1,8,256]{3,2,1,0:T(8,128)S(1)}, u32[]{:S(2)}, u32[]{:S(2)}) async-start(f32[4,1,8,256]{3,2,1,0:T(8,128)} %fusion.28), calls=%async_computation.3 | async-start | bytes 65536 | tf_op jit(solution)/shard_map/all_to_all | solution.py:220
  94.9 7.5 %collective-permute-start.4 = (f32[1,128]{1,0:T(1,128)S(1)}, f32[1,128]{1,0:T(1,128)S(1)}, u32[]{:S(2)}, u32[]{:S(2)}) collective-permute-start(f32[1,128]{1,0:T(1,128)S(1)} %slice.401), channel_id=1, source_target_pairs={{4,0},{8,4},{12,8},{5,1},{9,5},{13,9},{6,2},{10,6},{14,10},{7,3},{... | collective-permute-start | bytes 1544 | tf_op jit(solution)/shard_map/ppermute | solution.py:15
  96.2 6.2 %collective-permute-start.6 = (f32[64,1]{1,0:T(8,128)S(1)}, f32[64,1]{1,0:T(8,128)S(1)}, u32[]{:S(2)}, u32[]{:S(2)}) collective-permute-start(f32[64,1]{1,0:T(8,128)S(1)} %bitcast.268), channel_id=1, source_target_pairs={{1,0},{2,1},{3,2},{16,3},{17,16},{18,17},{19,18},{5,4},{6,5},{7,6}... | collective-permute-start | bytes 776 | tf_op jit(solution)/shard_map/ppermute | solution.py:15
  102.5 11.0 %collective-permute-start.5 = (f32[1,128]{1,0:T(1,128)S(1)}, f32[1,128]{1,0:T(1,128)S(1)}, u32[]{:S(2)}, u32[]{:S(2)}) collective-permute-start(f32[1,128]{1,0:T(1,128)S(1)} %slice.402), channel_id=1, source_target_pairs={{0,4},{4,8},{8,12},{1,5},{5,9},{9,13},{2,6},{6,10},{10,14},{3,7},{... | collective-permute-start | bytes 1544 | tf_op jit(solution)/shard_map/ppermute | solution.py:15
  107.1 6.4 %collective-permute-start.7 = (f32[64,1]{1,0:T(8,128)S(1)}, f32[64,1]{1,0:T(8,128)S(1)}, u32[]{:S(2)}, u32[]{:S(2)}) collective-permute-start(f32[64,1]{1,0:T(8,128)S(1)} %slice.406), channel_id=1, source_target_pairs={{0,1},{1,2},{2,3},{3,16},{16,17},{17,18},{18,19},{4,5},{5,6},{6,7}... | collective-permute-start | bytes 776 | tf_op jit(solution)/shard_map/ppermute | solution.py:15
  114.8 8.9 %all-to-all-start.4 = ((f32[1,1,32,256]{3,1,0,2:T(1,128)}), f32[1,1,32,256]{3,1,0,2:T(1,128)S(1)}, u32[]{:S(2)}, u32[]{:S(2)}) async-start(f32[1,1,32,256]{3,1,0,2:T(1,128)} %reshape.419), calls=%async_computation.4 | async-start | bytes 65536 | tf_op jit(solution)/shard_map/all_to_all | solution.py:195
  137.7 6.1 %collective-permute-start.10 = (f32[64,1]{1,0:T(8,128)S(1)}, f32[64,1]{1,0:T(8,128)S(1)}, u32[]{:S(2)}, u32[]{:S(2)}) collective-permute-start(f32[64,1]{1,0:T(8,128)S(1)} %bitcast.270), channel_id=1, source_target_pairs={{1,0},{2,1},{3,2},{16,3},{17,16},{18,17},{19,18},{5,4},{6,5},{7,6}... | collective-permute-start | bytes 776 | tf_op jit(solution)/shard_map/ppermute | solution.py:15
  139.0 5.5 %collective-permute-start.8 = (f32[1,128]{1,0:T(1,128)S(1)}, f32[1,128]{1,0:T(1,128)S(1)}, u32[]{:S(2)}, u32[]{:S(2)}) collective-permute-start(f32[1,128]{1,0:T(1,128)S(1)} %slice.421), channel_id=1, source_target_pairs={{4,0},{8,4},{12,8},{5,1},{9,5},{13,9},{6,2},{10,6},{14,10},{7,3},{... | collective-permute-start | bytes 1544 | tf_op jit(solution)/shard_map/ppermute | solution.py:15
  144.5 9.2 %copy-start.3 = (f32[64,128]{1,0:T(8,128)}, f32[64,128]{1,0:T(8,128)S(1)}, u32[]{:S(2)}) copy-start(f32[64,128]{1,0:T(8,128)S(1)} %get-tuple-element.78) | copy-start | bytes 98308
  144.6 9.2 %collective-permute-start.9 = (f32[1,128]{1,0:T(1,128)S(1)}, f32[1,128]{1,0:T(1,128)S(1)}, u32[]{:S(2)}, u32[]{:S(2)}) collective-permute-start(f32[1,128]{1,0:T(1,128)S(1)} %slice.422), channel_id=1, source_target_pairs={{0,4},{4,8},{8,12},{1,5},{5,9},{9,13},{2,6},{6,10},{10,14},{3,7},{... | collective-permute-start | bytes 1544 | tf_op jit(solution)/shard_map/ppermute | solution.py:15
  147.3 6.4 %collective-permute-start.11 = (f32[64,1]{1,0:T(8,128)S(1)}, f32[64,1]{1,0:T(8,128)S(1)}, u32[]{:S(2)}, u32[]{:S(2)}) collective-permute-start(f32[64,1]{1,0:T(8,128)S(1)} %slice.426), channel_id=1, source_target_pairs={{0,1},{1,2},{2,3},{3,16},{16,17},{17,18},{18,19},{4,5},{5,6},{6,7}... | collective-permute-start | bytes 776 | tf_op jit(solution)/shard_map/ppermute | solution.py:15
  155.0 8.9 %all-to-all-start.6 = ((f32[1,1,32,256]{3,1,0,2:T(1,128)}), f32[1,1,32,256]{3,1,0,2:T(1,128)S(1)}, u32[]{:S(2)}, u32[]{:S(2)}) async-start(f32[1,1,32,256]{3,1,0,2:T(1,128)} %reshape.420), calls=%async_computation.6 | async-start | bytes 65536 | tf_op jit(solution)/shard_map/all_to_all | solution.py:195
  170.2 8.9 %all-to-all-start.7 = ((f32[4,1,8,256]{3,2,1,0:T(8,128)}), f32[4,1,8,256]{3,2,1,0:T(8,128)S(1)}, u32[]{:S(2)}, u32[]{:S(2)}) async-start(f32[4,1,8,256]{3,2,1,0:T(8,128)} %fusion.32), calls=%async_computation.7 | async-start | bytes 65536 | tf_op jit(solution)/shard_map/all_to_all | solution.py:220
  179.4 41.5 %copy-start.9 = (f32[64,128]{1,0:T(8,128)}, f32[64,128]{1,0:T(8,128)S(1)}, u32[]{:S(2)}) copy-start(f32[64,128]{1,0:T(8,128)S(1)} %select_n.630) | copy-start | bytes 98308
  (12 other events, 36.8 us)
where the time goes:
time: 223 us; the launch traced here: 221 us
  starting transfers between devices  60.7 us (27%)
  blocking collectives  49.1 us (22%)
  waiting for transfers between devices  41.9 us (19%)
  between operations  32.9 us (15%)
  matrix products  15.9 us (7%)
  local copies, waits for them, and re-layouts  15.3 us (7%)
  other arithmetic  5.14 us (2%)
    psum x1, blocking collectives, shards(): traces = lax.psum(jnp.stack(samples), ('grp', 'gx', 'gy'))  41.1 us
    ppermute x12, starting transfers between devices, passed_along(): lax.ppermute(value, axis, [(source, source + steps) for source in range(i...  33.7 us
    all_to_all x3, waiting for transfers between devices, shards(): lax.all_to_all(to_flat_tiles(new), 'gx', split_axis=2, concat_axis=0, til...  15.8 us
    ppermute x12, waiting for transfers between devices, passed_along(): lax.ppermute(value, axis, [(source, source + steps) for source in range(i...  11.2 us
    all_to_all x2, waiting for transfers between devices, shards(): back = lax.all_to_all(means, 'gx', split_axis=0, concat_axis=2, tiled=True)  10.7 us
    all_to_all x3, starting transfers between devices, shards(): lax.all_to_all(to_flat_tiles(new), 'gx', split_axis=2, concat_axis=0, til...  9.97 us
    dot_general x9, matrix products, fine_round(): jnp.dot(mixed, spread, precision=lax.Precision.HIGHEST, preferred_element...  9.19 us
    all_to_all x1, blocking collectives, shards(): back = lax.all_to_all(means, 'gx', split_axis=0, concat_axis=2, tiled=True)  8.01 us
  transfers between devices with their start and end apart: 19, of which 11 were waited for; matrix products, arithmetic and copies ran while one was open for 5% of the time, Pallas kernels for 0%

commit v1 on v0

--- a/solution.py
+++ b/solution.py
@@ -223,7 +223,7 @@
             rcv_rows, ez, precision=lax.Precision.HIGHEST, preferred_element_type=jnp.float32
         )
         samples.append(jnp.sum(picked * rcv_cols, axis=1))
-    traces = lax.psum(jnp.stack(samples), ("grp", "gx", "gy"))
+    traces = jnp.sum(lax.all_gather(jnp.stack(samples), ("grp", "gx", "gy")), axis=0)
     return (
         ez,
         hx,

time: 223 us -> 249 us (1.12)
  blocking collectives: 49.1 us -> 74.6 us
    all_gather x0 -> x1, blocking collectives: none -> 66.6 us  [shards(): lax.all_gather(jnp.stack(samples), ('grp', 'gx', 'gy'))]
    psum x1 -> x0, blocking collectives: 41.1 us -> none  [shards(): traces = lax.psum(jnp.stack(samples), ('grp', 'gx', 'gy'))]
where the time goes in v1:
time: 249 us; the launch traced here: 247 us
  blocking collectives  74.6 us (30%)
  starting transfers between devices  60.7 us (24%)
  waiting for transfers between devices  41.9 us (17%)
  between operations  32.8 us (13%)
  matrix products  15.9 us (6%)
  local copies, waits for them, and re-layouts  15.3 us (6%)
  other arithmetic  5.76 us (2%)
    all_gather x1, blocking collectives, shards(): lax.all_gather(jnp.stack(samples), ('grp', 'gx', 'gy'))  66.6 us
    ppermute x12, starting transfers between devices, passed_along(): lax.ppermute(value, axis, [(source, source + steps) for source in range(i...  33.7 us
    all_to_all x3, waiting for transfers between devices, shards(): lax.all_to_all(to_flat_tiles(new), 'gx', split_axis=2, concat_axis=0, til...  15.8 us
    ppermute x12, waiting for transfers between devices, passed_along(): lax.ppermute(value, axis, [(source, source + steps) for source in range(i...  11.2 us
    all_to_all x2, waiting for transfers between devices, shards(): back = lax.all_to_all(means, 'gx', split_axis=0, concat_axis=2, tiled=True)  10.7 us
    all_to_all x3, starting transfers between devices, shards(): lax.all_to_all(to_flat_tiles(new), 'gx', split_axis=2, concat_axis=0, til...  9.97 us
    dot_general x9, matrix products, fine_round(): jnp.dot(mixed, spread, precision=lax.Precision.HIGHEST, preferred_element...  9.19 us
    all_to_all x1, blocking collectives, shards(): back = lax.all_to_all(means, 'gx', split_axis=0, concat_axis=2, tiled=True)  8.01 us
  transfers between devices with their start and end apart: 19, of which 11 were waited for; matrix products, arithmetic and copies ran while one was open for 5% of the time, Pallas kernels for 0%

profile of v1, /device:TPU:0, one launch (start us, length us, event | category | flops | bytes accessed | tf_op | source)
XLA Modules:
  0.0 247.0 jit_solution(6950932597651475403)
XLA Ops:
  2.1 6.3 %all-to-all-start = ((s32[1,1,32,4]{3,1,0,2:T(1,128)}), s32[1,1,32,4]{3,1,0,2:T(1,128)S(1)}, u32[]{:S(2)}, u32[]{:S(2)}) async-start(s32[1,1,32,4]{3,1,0,2:T(1,128)} %copy.34), calls=%async_computation | async-start | bytes 32768 | tf_op jit(solution)/shard_map/all_to_all | solution.py:158
  51.5 4.6 %collective-permute-start.1 = (f32[1,128]{1,0:T(1,128)S(1)}, f32[1,128]{1,0:T(1,128)S(1)}, u32[]{:S(2)}, u32[]{:S(2)}) collective-permute-start(f32[1,128]{1,0:T(1,128)S(1)} %slice.384), channel_id=1, source_target_pairs={{0,4},{4,8},{8,12},{1,5},{5,9},{9,13},{2,6},{6,10},{10,14},{3,7},{... | collective-permute-start | bytes 1544 | tf_op jit(solution)/shard_map/ppermute | solution.py:15
  56.1 4.6 %collective-permute-start.3 = (f32[64,1]{1,0:T(8,128)S(1)}, f32[64,1]{1,0:T(8,128)S(1)}, u32[]{:S(2)}, u32[]{:S(2)}) collective-permute-start(f32[64,1]{1,0:T(8,128)S(1)} %slice.386), channel_id=1, source_target_pairs={{0,1},{1,2},{2,3},{3,16},{16,17},{17,18},{18,19},{4,5},{5,6},{6,7}... | collective-permute-start | bytes 776 | tf_op jit(solution)/shard_map/ppermute | solution.py:15
  60.7 4.2 %all-to-all-start.1 = ((f32[1,1,32,256]{3,1,0,2:T(1,128)}), f32[1,1,32,256]{3,1,0,2:T(1,128)S(1)}, u32[]{:S(2)}, u32[]{:S(2)}) async-start(f32[1,1,32,256]{3,1,0,2:T(1,128)} %reshape.421), calls=%async_computation.1 | async-start | bytes 65536 | tf_op jit(solution)/shard_map/all_to_all | solution.py:180
  66.3 4.3 %all-to-all-done.1 = f32[1,1,32,256]{3,1,0,2:T(1,128)S(1)} async-done(((f32[1,1,32,256]{3,1,0,2:T(1,128)}), f32[1,1,32,256]{3,1,0,2:T(1,128)S(1)}, u32[]{:S(2)}, u32[]{:S(2)}) %all-to-all-start.1) | async-done | bytes 32800 | tf_op jit(solution)/shard_map/all_to_all | solution.py:180
  70.5 3.3 %all-to-all-start.2 = ((f32[1,1,32,256]{3,1,0,2:T(1,128)}), f32[1,1,32,256]{3,1,0,2:T(1,128)S(1)}, u32[]{:S(2)}, u32[]{:S(2)}) async-start(f32[1,1,32,256]{3,1,0,2:T(1,128)} %reshape.422), calls=%async_computation.2 | async-start | bytes 65536 | tf_op jit(solution)/shard_map/all_to_all | solution.py:195
  74.1 5.3 %all-to-all-done.2 = f32[1,1,32,256]{3,1,0,2:T(1,128)S(1)} async-done(((f32[1,1,32,256]{3,1,0,2:T(1,128)}), f32[1,1,32,256]{3,1,0,2:T(1,128)S(1)}, u32[]{:S(2)}, u32[]{:S(2)}) %all-to-all-start.2) | async-done | bytes 32800 | tf_op jit(solution)/shard_map/all_to_all | solution.py:195
  83.8 1.8 fusion.28
  85.6 3.3 %all-to-all-start.3 = ((f32[4,1,8,256]{3,2,1,0:T(8,128)}), f32[4,1,8,256]{3,2,1,0:T(8,128)S(1)}, u32[]{:S(2)}, u32[]{:S(2)}) async-start(f32[4,1,8,256]{3,2,1,0:T(8,128)} %fusion.28), calls=%async_computation.3 | async-start | bytes 65536 | tf_op jit(solution)/shard_map/all_to_all | solution.py:220
  89.2 5.3 %all-to-all-done.3 = f32[4,1,8,256]{3,2,1,0:T(8,128)S(1)} async-done(((f32[4,1,8,256]{3,2,1,0:T(8,128)}), f32[4,1,8,256]{3,2,1,0:T(8,128)S(1)}, u32[]{:S(2)}, u32[]{:S(2)}) %all-to-all-start.3) | async-done | bytes 32800 | tf_op jit(solution)/shard_map/all_to_all | solution.py:220
  97.6 4.8 %collective-permute-done.6 = f32[64,1]{1,0:T(8,128)S(1)} collective-permute-done((f32[64,1]{1,0:T(8,128)S(1)}, f32[64,1]{1,0:T(8,128)S(1)}, u32[]{:S(2)}, u32[]{:S(2)}) %collective-permute-start.6) | collective-permute-done | bytes 288 | tf_op jit(solution)/shard_map/ppermute | solution.py:15
  102.5 4.5 %collective-permute-start.5 = (f32[1,128]{1,0:T(1,128)S(1)}, f32[1,128]{1,0:T(1,128)S(1)}, u32[]{:S(2)}, u32[]{:S(2)}) collective-permute-start(f32[1,128]{1,0:T(1,128)S(1)} %slice.402), channel_id=1, source_target_pairs={{0,4},{4,8},{8,12},{1,5},{5,9},{9,13},{2,6},{6,10},{10,14},{3,7},{... | collective-permute-start | bytes 1544 | tf_op jit(solution)/shard_map/ppermute | solution.py:15
  107.1 4.8 %collective-permute-start.7 = (f32[64,1]{1,0:T(8,128)S(1)}, f32[64,1]{1,0:T(8,128)S(1)}, u32[]{:S(2)}, u32[]{:S(2)}) collective-permute-start(f32[64,1]{1,0:T(8,128)S(1)} %slice.406), channel_id=1, source_target_pairs={{0,1},{1,2},{2,3},{3,16},{16,17},{17,18},{18,19},{4,5},{5,6},{6,7}... | collective-permute-start | bytes 776 | tf_op jit(solution)/shard_map/ppermute | solution.py:15
  114.8 3.4 %all-to-all-start.4 = ((f32[1,1,32,256]{3,1,0,2:T(1,128)}), f32[1,1,32,256]{3,1,0,2:T(1,128)S(1)}, u32[]{:S(2)}, u32[]{:S(2)}) async-start(f32[1,1,32,256]{3,1,0,2:T(1,128)} %reshape.423), calls=%async_computation.4 | async-start | bytes 65536 | tf_op jit(solution)/shard_map/all_to_all | solution.py:195
  118.5 5.2 %all-to-all-done.4 = f32[1,1,32,256]{3,1,0,2:T(1,128)S(1)} async-done(((f32[1,1,32,256]{3,1,0,2:T(1,128)}), f32[1,1,32,256]{3,1,0,2:T(1,128)S(1)}, u32[]{:S(2)}, u32[]{:S(2)}) %all-to-all-start.4) | async-done | bytes 32800 | tf_op jit(solution)/shard_map/all_to_all | solution.py:195
  129.3 8.0 %all_to_all.32 = f32[4,1,8,256]{3,2,1,0:T(8,128)S(1)} all-to-all(f32[4,1,8,256]{3,2,1,0:T(8,128)S(1)} %fusion.30), channel_id=1, replica_groups=mesh['grp'=2,'gx'=4,'gy'=4] {'gx'}, dimensions={0} | all-to-all | bytes 65536 | tf_op jit(solution)/shard_map/all_to_all | solution.py:220
  140.4 3.4 %collective-permute-done.10 = f32[64,1]{1,0:T(8,128)S(1)} collective-permute-done((f32[64,1]{1,0:T(8,128)S(1)}, f32[64,1]{1,0:T(8,128)S(1)}, u32[]{:S(2)}, u32[]{:S(2)}) %collective-permute-start.10) | collective-permute-done | bytes 288 | tf_op jit(solution)/shard_map/ppermute | solution.py:15
  144.6 2.6 %collective-permute-start.9 = (f32[1,128]{1,0:T(1,128)S(1)}, f32[1,128]{1,0:T(1,128)S(1)}, u32[]{:S(2)}, u32[]{:S(2)}) collective-permute-start(f32[1,128]{1,0:T(1,128)S(1)} %slice.422), channel_id=1, source_target_pairs={{0,4},{4,8},{8,12},{1,5},{5,9},{9,13},{2,6},{6,10},{10,14},{3,7},{... | collective-permute-start | bytes 1544 | tf_op jit(solution)/shard_map/ppermute | solution.py:15
  147.3 4.8 %collective-permute-start.11 = (f32[64,1]{1,0:T(8,128)S(1)}, f32[64,1]{1,0:T(8,128)S(1)}, u32[]{:S(2)}, u32[]{:S(2)}) collective-permute-start(f32[64,1]{1,0:T(8,128)S(1)} %slice.426), channel_id=1, source_target_pairs={{0,1},{1,2},{2,3},{3,16},{16,17},{17,18},{18,19},{4,5},{5,6},{6,7}... | collective-permute-start | bytes 776 | tf_op jit(solution)/shard_map/ppermute | solution.py:15
  155.0 3.3 %all-to-all-start.6 = ((f32[1,1,32,256]{3,1,0,2:T(1,128)}), f32[1,1,32,256]{3,1,0,2:T(1,128)S(1)}, u32[]{:S(2)}, u32[]{:S(2)}) async-start(f32[1,1,32,256]{3,1,0,2:T(1,128)} %reshape.424), calls=%async_computation.6 | async-start | bytes 65536 | tf_op jit(solution)/shard_map/all_to_all | solution.py:195
  158.6 5.4 %all-to-all-done.6 = f32[1,1,32,256]{3,1,0,2:T(1,128)S(1)} async-done(((f32[1,1,32,256]{3,1,0,2:T(1,128)}), f32[1,1,32,256]{3,1,0,2:T(1,128)S(1)}, u32[]{:S(2)}, u32[]{:S(2)}) %all-to-all-start.6) | async-done | bytes 32800 | tf_op jit(solution)/shard_map/all_to_all | solution.py:195
  170.2 3.3 %all-to-all-start.7 = ((f32[4,1,8,256]{3,2,1,0:T(8,128)}), f32[4,1,8,256]{3,2,1,0:T(8,128)S(1)}, u32[]{:S(2)}, u32[]{:S(2)}) async-start(f32[4,1,8,256]{3,2,1,0:T(8,128)} %fusion.32), calls=%async_computation.7 | async-start | bytes 65536 | tf_op jit(solution)/shard_map/all_to_all | solution.py:220
  173.8 5.3 %all-to-all-done.7 = f32[4,1,8,256]{3,2,1,0:T(8,128)S(1)} async-done(((f32[4,1,8,256]{3,2,1,0:T(8,128)}), f32[4,1,8,256]{3,2,1,0:T(8,128)S(1)}, u32[]{:S(2)}, u32[]{:S(2)}) %all-to-all-start.7) | async-done | bytes 32800 | tf_op jit(solution)/shard_map/all_to_all | solution.py:220
  179.8 66.6 %all-gather.1 = f32[32,3,128]{2,1,0:T(4,128)S(1)} all-gather(f32[1,3,128]{2,1,0:T(4,128)S(1)} %maximum_bitcast_fusion), channel_id=2, replica_groups=mesh['grp'=2,'gx'=4,'gy'=4] {'grp','gx','gy'}, dimensions={0}, use_global_device_ids=true | all-gather | bytes 50688 | tf_op jit(solution)/shard_map/all_gather | solution.py:226
  (167 shorter events, 45.8 us)
Async XLA Ops:
  0.6 46.8 %copy-start.13 = (f32[3,4]{1,0:T(4,128)S(1)}, f32[3,4]{1,0:T(4,128)}, u32[]{:S(2)}) copy-start(f32[3,4]{1,0:T(4,128)} %param.26) | copy-start | bytes 148
  0.6 46.9 %copy-start.14 = (s32[4]{0:T(128)S(1)}, s32[4]{0:T(128)}, u32[]{:S(2)}) copy-start(s32[4]{0:T(128)} %param.25) | copy-start | bytes 52
  0.7 47.0 %copy-start.4 = (s32[4,1,8,2304]{3,2,1,0:T(8,128)S(1)}, s32[4,1,8,2304]{3,2,1,0:T(8,128)}, u32[]{:S(2)}) copy-start(s32[4,1,8,2304]{3,2,1,0:T(8,128)} %param.23) | copy-start | bytes 884740
  2.1 58.6 %all-to-all-start = ((s32[1,1,32,4]{3,1,0,2:T(1,128)}), s32[1,1,32,4]{3,1,0,2:T(1,128)S(1)}, u32[]{:S(2)}, u32[]{:S(2)}) async-start(s32[1,1,32,4]{3,1,0,2:T(1,128)} %copy.34), calls=%async_computation | async-start | bytes 32768 | tf_op jit(solution)/shard_map/all_to_all | solution.py:158
  8.4 42.9 %collective-permute-start.2 = (f32[64,1]{1,0:T(8,128)}, f32[64,1]{1,0:T(8,128)S(1)}, u32[]{:S(2)}, u32[]{:S(2)}) collective-permute-start(f32[64,1]{1,0:T(8,128)} %bitcast.269), channel_id=1, source_target_pairs={{1,0},{2,1},{3,2},{16,3},{17,16},{18,17},{19,18},{5,4},{6,5},{7,6}... | collective-permute-start | bytes 776 | tf_op jit(solution)/shard_map/ppermute | solution.py:15
  10.4 41.0 %collective-permute-start = (f32[1,128]{1,0:T(1,128)S(1)}, f32[1,128]{1,0:T(1,128)S(1)}, u32[]{:S(2)}, u32[]{:S(2)}) collective-permute-start(f32[1,128]{1,0:T(1,128)S(1)} %slice.322), channel_id=1, source_target_pairs={{4,0},{8,4},{12,8},{5,1},{9,5},{13,9},{6,2},{10,6},{14,10},{7,3},{... | collective-permute-start | bytes 1544 | tf_op jit(solution)/shard_map/ppermute | solution.py:15
  51.5 13.5 %collective-permute-start.1 = (f32[1,128]{1,0:T(1,128)S(1)}, f32[1,128]{1,0:T(1,128)S(1)}, u32[]{:S(2)}, u32[]{:S(2)}) collective-permute-start(f32[1,128]{1,0:T(1,128)S(1)} %slice.384), channel_id=1, source_target_pairs={{0,4},{4,8},{8,12},{1,5},{5,9},{9,13},{2,6},{6,10},{10,14},{3,7},{... | collective-permute-start | bytes 1544 | tf_op jit(solution)/shard_map/ppermute | solution.py:15
  56.1 8.9 %collective-permute-start.3 = (f32[64,1]{1,0:T(8,128)S(1)}, f32[64,1]{1,0:T(8,128)S(1)}, u32[]{:S(2)}, u32[]{:S(2)}) collective-permute-start(f32[64,1]{1,0:T(8,128)S(1)} %slice.386), channel_id=1, source_target_pairs={{0,1},{1,2},{2,3},{3,16},{16,17},{17,18},{18,19},{4,5},{5,6},{6,7}... | collective-permute-start | bytes 776 | tf_op jit(solution)/shard_map/ppermute | solution.py:15
  60.7 9.9 %all-to-all-start.1 = ((f32[1,1,32,256]{3,1,0,2:T(1,128)}), f32[1,1,32,256]{3,1,0,2:T(1,128)S(1)}, u32[]{:S(2)}, u32[]{:S(2)}) async-start(f32[1,1,32,256]{3,1,0,2:T(1,128)} %reshape.421), calls=%async_computation.1 | async-start | bytes 65536 | tf_op jit(solution)/shard_map/all_to_all | solution.py:180
  70.5 8.9 %all-to-all-start.2 = ((f32[1,1,32,256]{3,1,0,2:T(1,128)}), f32[1,1,32,256]{3,1,0,2:T(1,128)S(1)}, u32[]{:S(2)}, u32[]{:S(2)}) async-start(f32[1,1,32,256]{3,1,0,2:T(1,128)} %reshape.422), calls=%async_computation.2 | async-start | bytes 65536 | tf_op jit(solution)/shard_map/all_to_all | solution.py:195
  85.6 8.9 %all-to-all-start.3 = ((f32[4,1,8,256]{3,2,1,0:T(8,128)}), f32[4,1,8,256]{3,2,1,0:T(8,128)S(1)}, u32[]{:S(2)}, u32[]{:S(2)}) async-start(f32[4,1,8,256]{3,2,1,0:T(8,128)} %fusion.28), calls=%async_computation.3 | async-start | bytes 65536 | tf_op jit(solution)/shard_map/all_to_all | solution.py:220
  94.9 7.5 %collective-permute-start.4 = (f32[1,128]{1,0:T(1,128)S(1)}, f32[1,128]{1,0:T(1,128)S(1)}, u32[]{:S(2)}, u32[]{:S(2)}) collective-permute-start(f32[1,128]{1,0:T(1,128)S(1)} %slice.401), channel_id=1, source_target_pairs={{4,0},{8,4},{12,8},{5,1},{9,5},{13,9},{6,2},{10,6},{14,10},{7,3},{... | collective-permute-start | bytes 1544 | tf_op jit(solution)/shard_map/ppermute | solution.py:15
  96.2 6.2 %collective-permute-start.6 = (f32[64,1]{1,0:T(8,128)S(1)}, f32[64,1]{1,0:T(8,128)S(1)}, u32[]{:S(2)}, u32[]{:S(2)}) collective-permute-start(f32[64,1]{1,0:T(8,128)S(1)} %bitcast.270), channel_id=1, source_target_pairs={{1,0},{2,1},{3,2},{16,3},{17,16},{18,17},{19,18},{5,4},{6,5},{7,6}... | collective-permute-start | bytes 776 | tf_op jit(solution)/shard_map/ppermute | solution.py:15
  102.5 11.0 %collective-permute-start.5 = (f32[1,128]{1,0:T(1,128)S(1)}, f32[1,128]{1,0:T(1,128)S(1)}, u32[]{:S(2)}, u32[]{:S(2)}) collective-permute-start(f32[1,128]{1,0:T(1,128)S(1)} %slice.402), channel_id=1, source_target_pairs={{0,4},{4,8},{8,12},{1,5},{5,9},{9,13},{2,6},{6,10},{10,14},{3,7},{... | collective-permute-start | bytes 1544 | tf_op jit(solution)/shard_map/ppermute | solution.py:15
  107.1 6.4 %collective-permute-start.7 = (f32[64,1]{1,0:T(8,128)S(1)}, f32[64,1]{1,0:T(8,128)S(1)}, u32[]{:S(2)}, u32[]{:S(2)}) collective-permute-start(f32[64,1]{1,0:T(8,128)S(1)} %slice.406), channel_id=1, source_target_pairs={{0,1},{1,2},{2,3},{3,16},{16,17},{17,18},{18,19},{4,5},{5,6},{6,7}... | collective-permute-start | bytes 776 | tf_op jit(solution)/shard_map/ppermute | solution.py:15
  114.8 8.9 %all-to-all-start.4 = ((f32[1,1,32,256]{3,1,0,2:T(1,128)}), f32[1,1,32,256]{3,1,0,2:T(1,128)S(1)}, u32[]{:S(2)}, u32[]{:S(2)}) async-start(f32[1,1,32,256]{3,1,0,2:T(1,128)} %reshape.423), calls=%async_computation.4 | async-start | bytes 65536 | tf_op jit(solution)/shard_map/all_to_all | solution.py:195
  137.7 6.1 %collective-permute-start.10 = (f32[64,1]{1,0:T(8,128)S(1)}, f32[64,1]{1,0:T(8,128)S(1)}, u32[]{:S(2)}, u32[]{:S(2)}) collective-permute-start(f32[64,1]{1,0:T(8,128)S(1)} %bitcast.272), channel_id=1, source_target_pairs={{1,0},{2,1},{3,2},{16,3},{17,16},{18,17},{19,18},{5,4},{6,5},{7,6}... | collective-permute-start | bytes 776 | tf_op jit(solution)/shard_map/ppermute | solution.py:15
  139.0 5.5 %collective-permute-start.8 = (f32[1,128]{1,0:T(1,128)S(1)}, f32[1,128]{1,0:T(1,128)S(1)}, u32[]{:S(2)}, u32[]{:S(2)}) collective-permute-start(f32[1,128]{1,0:T(1,128)S(1)} %slice.421), channel_id=1, source_target_pairs={{4,0},{8,4},{12,8},{5,1},{9,5},{13,9},{6,2},{10,6},{14,10},{7,3},{... | collective-permute-start | bytes 1544 | tf_op jit(solution)/shard_map/ppermute | solution.py:15
  144.5 9.2 %copy-start.3 = (f32[64,128]{1,0:T(8,128)}, f32[64,128]{1,0:T(8,128)S(1)}, u32[]{:S(2)}) copy-start(f32[64,128]{1,0:T(8,128)S(1)} %get-tuple-element.78) | copy-start | bytes 98308
  144.6 9.2 %collective-permute-start.9 = (f32[1,128]{1,0:T(1,128)S(1)}, f32[1,128]{1,0:T(1,128)S(1)}, u32[]{:S(2)}, u32[]{:S(2)}) collective-permute-start(f32[1,128]{1,0:T(1,128)S(1)} %slice.422), channel_id=1, source_target_pairs={{0,4},{4,8},{8,12},{1,5},{5,9},{9,13},{2,6},{6,10},{10,14},{3,7},{... | collective-permute-start | bytes 1544 | tf_op jit(solution)/shard_map/ppermute | solution.py:15
  147.3 6.4 %collective-permute-start.11 = (f32[64,1]{1,0:T(8,128)S(1)}, f32[64,1]{1,0:T(8,128)S(1)}, u32[]{:S(2)}, u32[]{:S(2)}) collective-permute-start(f32[64,1]{1,0:T(8,128)S(1)} %slice.426), channel_id=1, source_target_pairs={{0,1},{1,2},{2,3},{3,16},{16,17},{17,18},{18,19},{4,5},{5,6},{6,7}... | collective-permute-start | bytes 776 | tf_op jit(solution)/shard_map/ppermute | solution.py:15
  155.0 8.9 %all-to-all-start.6 = ((f32[1,1,32,256]{3,1,0,2:T(1,128)}), f32[1,1,32,256]{3,1,0,2:T(1,128)S(1)}, u32[]{:S(2)}, u32[]{:S(2)}) async-start(f32[1,1,32,256]{3,1,0,2:T(1,128)} %reshape.424), calls=%async_computation.6 | async-start | bytes 65536 | tf_op jit(solution)/shard_map/all_to_all | solution.py:195
  170.2 8.9 %all-to-all-start.7 = ((f32[4,1,8,256]{3,2,1,0:T(8,128)}), f32[4,1,8,256]{3,2,1,0:T(8,128)S(1)}, u32[]{:S(2)}, u32[]{:S(2)}) async-start(f32[4,1,8,256]{3,2,1,0:T(8,128)} %fusion.32), calls=%async_computation.7 | async-start | bytes 65536 | tf_op jit(solution)/shard_map/all_to_all | solution.py:220
  179.4 67.6 %copy-start.9 = (f32[64,128]{1,0:T(8,128)}, f32[64,128]{1,0:T(8,128)S(1)}, u32[]{:S(2)}) copy-start(f32[64,128]{1,0:T(8,128)S(1)} %select_n.630) | copy-start | bytes 98308
  (12 other events, 36.8 us)
